TPU v7x, 256 devices: a whole 4x4x8 slice. The times are simulated.
256 devices in a mesh: act: 64 (over x, z, core), rep: 4 (over y).
Axes of the slice: x: 4, y: 4, z: 8, core: 2. Of those that a mesh axis runs over, the one named last changes fastest.
Arguments:
- estimated_returns: float32 [512, 131072], P('act', 'rep'), may hold values from -1000 to 1000
- chosen_move_ids: int32 [512, 131072], P('act', 'rep'), may hold values from 0 to 17
- previous_eta: float32 [1], replicated, may hold values from 0.3 to 3
- trust_region_epsilon: float32 [1], replicated, may hold values from 0.02 to 1
Outputs:
- sample_importance: float32 [512, 131072], P('act', 'rep')
- goal_distribution: float32 [18, 131072], P(None, ('rep', 'act'))
- new_temperature: float32 [1], replicated
All inputs are finite; a program needn't handle non-finite values.
Results may differ from a plain program's by a relative error of at most 0.0003.
Values sent between devices are 32-bit elements; how exact they have to be, the bound alone decides.
No kernel may reach another device: no remote copies, remote signals or barrier semaphores. Data moves between devices by JAX's collectives and lax.ppermute only.
A program may use at most 64 MiB of HBM per device.

v0:
```python
import jax
import jax.numpy as jnp
from jax import lax
from jax.sharding import Mesh
from jax.sharding import PartitionSpec as P

NACT = 18
ITERS = 3
ACT = ("act_0", "act_1", "act_2")
REP_ACT = ("rep", "act_0", "act_1", "act_2")


def cut_along(shard, dim, peers):
    shape = shard.shape
    blocks = shard.reshape(*shape[:dim], peers, shape[dim] // peers, *shape[dim + 1 :])
    return jnp.moveaxis(blocks, dim, 0)


def sum_at_owner(shard, axis, dim):
    blocks = cut_along(shard, dim, lax.axis_size(axis))
    arrived = lax.all_to_all(blocks, axis, split_axis=0, concat_axis=0, tiled=True)
    return arrived.sum(axis=0)


def sum_in_two_steps(shard, axes, dim):
    far, near = axes
    own = sum_at_owner(cut_along(shard, dim, lax.axis_size(far)), near, dim + 1)
    return jnp.sum(lax.all_to_all(own, far, 0, 0, tiled=True), axis=0)


def copy_for_each(shard, axis):
    copies = jnp.broadcast_to(shard, (lax.axis_size(axis), *shard.shape))
    return lax.all_to_all(copies, axis, split_axis=0, concat_axis=0, tiled=True)


def over_copies(shard, axis):
    everything = copy_for_each(shard, axis)
    return jnp.sum(everything, axis=0)


def by_axis(shard, axes):
    far, near = axes
    return over_copies(over_copies(shard, near), far)


def together(arrays, axis):
    ends = [0]
    for a in arrays:
        ends.append(ends[-1] + a.size)
    total = by_axis(jnp.concatenate([a.ravel() for a in arrays]), axis)
    return tuple((total[b:e].reshape(a.shape) for a, b, e in zip(arrays, ends, ends[1:])))


def summary_figures(centered_returns, lagrange_eta):
    exponential_term = jnp.exp(centered_returns / lagrange_eta)
    partition_total = jnp.sum(exponential_term, axis=0)
    leading_part = jnp.sum(exponential_term * centered_returns, axis=0)
    trailing_part = jnp.sum(exponential_term * centered_returns * centered_returns, axis=0)
    return (exponential_term, partition_total, leading_part, trailing_part)


def within_situation(partition_total, leading_part, trailing_part, lagrange_eta, move_draws):
    entropy_gap = (
        leading_part / (partition_total * lagrange_eta)
        - jnp.log(partition_total)
        + jnp.log(jnp.float32(move_draws))
    )
    mean_first = leading_part / partition_total
    spread = trailing_part / partition_total - mean_first * mean_first
    return (jnp.sum(entropy_gap), jnp.sum(spread))


def gradient_step(lagrange_eta, ceiling_term, aggregate_relative_entropy, aggregate_deviation):
    change_amount = (
        (ceiling_term - aggregate_relative_entropy)
        * lagrange_eta
        / (1.0 + aggregate_deviation / lagrange_eta)
    )
    return lagrange_eta * jnp.exp(-jnp.tanh(change_amount))


def per_action(probs, ids_block):
    return jnp.stack([jnp.sum(jnp.where(ids_block == k, probs, 0.0), axis=0) for k in range(NACT)])


def scatter_target(probs, ids_block):
    return sum_in_two_steps(per_action(probs, ids_block), (("act_0", "act_1"), "act_2"), 1)


def on_device(estimated_returns, chosen_move_ids, previous_eta, trust_region_epsilon):
    lagrange_eta = previous_eta[0]
    ceiling_term = trust_region_epsilon[0]
    move_draws = estimated_returns.shape[0] * lax.axis_size(ACT)
    q_rows = lax.all_to_all(estimated_returns, ACT, split_axis=1, concat_axis=0, tiled=True)
    tally_number = q_rows.shape[1] * lax.axis_size(ACT) * lax.axis_size("rep")
    centered_returns = q_rows - jnp.max(q_rows, axis=0, keepdims=True)
    for step in range(ITERS):
        exponential_term, partition_total, leading_part, trailing_part = summary_figures(
            centered_returns, lagrange_eta
        )
        shard_divergence, shard_value_spread = within_situation(
            partition_total, leading_part, trailing_part, lagrange_eta, move_draws
        )
        aggregate_relative_entropy, aggregate_deviation = together(
            (shard_divergence, shard_value_spread), (("act_0", "act_1"), ("act_2", "rep"))
        )
        lagrange_eta = gradient_step(
            lagrange_eta,
            ceiling_term,
            aggregate_relative_entropy / tally_number,
            aggregate_deviation / tally_number,
        )
    exponential_term, partition_total, leading_part, trailing_part = summary_figures(
        centered_returns, lagrange_eta
    )
    probs_rows = exponential_term / partition_total
    sample_importance = lax.all_to_all(
        move_draws * probs_rows, ACT, split_axis=0, concat_axis=1, tiled=True
    )
    goal_distribution = scatter_target(sample_importance / jnp.float32(move_draws), chosen_move_ids)
    return (sample_importance, goal_distribution, jnp.reshape(lagrange_eta, (1,)))


def solution(mesh):
    split = Mesh(
        mesh.devices.reshape(4, 8, 2, mesh.shape["rep"]), ("act_0", "act_1", "act_2", "rep")
    )
    placed = (P(ACT, "rep"), P(ACT, "rep"), P(), P())
    return jax.shard_map(
        on_device,
        mesh=split,
        in_specs=placed,
        out_specs=(P(ACT, "rep"), P(None, REP_ACT), P()),
        check_vma=False,
    )
```

profile of v0, /device:TPU:32, one launch (start us, length us, event | category | flops | bytes accessed | tf_op | source)
XLA Modules:
  0.0 227.9 jit_solution(15470701140509389967)
XLA Ops:
  0.6 11.6 %all-to-all-start = ((f32[8,64,512]{2,0,1:T(8,128)}), f32[8,64,512]{2,0,1:T(8,128)S(1)}, u32[]{:S(2)}, u32[]{:S(2)}) async-start(f32[8,64,512]{2,0,1:T(8,128)} %bitcast.90), calls=%async_computation | async-start | bytes 2097152 | tf_op jit(solution)/shard_map/all_to_all | solution.py:94
  12.9 27.2 %all-to-all-done = f32[8,64,512]{2,0,1:T(8,128)S(1)} async-done(((f32[8,64,512]{2,0,1:T(8,128)}), f32[8,64,512]{2,0,1:T(8,128)S(1)}, u32[]{:S(2)}, u32[]{:S(2)}) %all-to-all-start) | async-done | bytes 1048608 | tf_op jit(solution)/shard_map/all_to_all | solution.py:94
  40.2 0.3 fusion.1
  40.5 0.6 add_reduce_fusion.2
  41.2 1.4 pad_maximum_fusion
  42.5 9.5 %all_to_all.75 = f32[8,1,2]{2,1,0:T(1,128)S(1)} all-to-all(f32[8,1,2]{2,1,0:T(1,128)S(1)} %broadcast_in_dim.41), channel_id=1, replica_groups=mesh['act_0'=4,'act_1'=8,'act_2'=2,'rep'=4] {'act_2','rep'}, dimensions={0} | all-to-all | bytes 128 | tf_op jit(solution)/shard_map/all_to_all | solution.py:33
  52.1 0.6 broadcast_in_dim.42
  52.7 6.5 %all-to-all-start.2 = ((f32[32,1,2]{2,1,0:T(1,128)}), f32[32,1,2]{2,1,0:T(1,128)S(1)}, u32[]{:S(2)}, u32[]{:S(2)}) async-start(f32[32,1,2]{2,1,0:T(1,128)} %broadcast_in_dim.42), calls=%async_computation.2 | async-start | bytes 32768 | tf_op jit(solution)/shard_map/all_to_all | solution.py:33
  59.8 7.9 %all-to-all-done.2 = f32[32,1,2]{2,1,0:T(1,128)S(1)} async-done(((f32[32,1,2]{2,1,0:T(1,128)}), f32[32,1,2]{2,1,0:T(1,128)S(1)}, u32[]{:S(2)}, u32[]{:S(2)}) %all-to-all-start.2) | async-done | bytes 288 | tf_op jit(solution)/shard_map/all_to_all | solution.py:33
  67.8 0.6 fusion.16
  69.9 0.3 fusion.3
  70.2 0.6 add_reduce_fusion.1
  70.8 1.4 pad_maximum_fusion.1
  72.2 7.6 %all_to_all.76 = f32[8,1,2]{2,1,0:T(1,128)S(1)} all-to-all(f32[8,1,2]{2,1,0:T(1,128)S(1)} %broadcast_in_dim.43), channel_id=1, replica_groups=mesh['act_0'=4,'act_1'=8,'act_2'=2,'rep'=4] {'act_2','rep'}, dimensions={0} | all-to-all | bytes 128 | tf_op jit(solution)/shard_map/all_to_all | solution.py:33
  79.8 12.8 %all_to_all.77 = f32[32,1,2]{2,1,0:T(1,128)S(1)} all-to-all(f32[32,1,2]{2,1,0:T(1,128)S(1)} %broadcast_in_dim.44), channel_id=1, replica_groups=mesh['act_0'=4,'act_1'=8,'act_2'=2,'rep'=4] {'act_0','act_1'}, dimensions={0} | all-to-all | bytes 512 | tf_op jit(solution)/shard_map/all_to_all | solution.py:33
  92.7 0.6 fusion.15
  95.1 0.6 add_reduce_fusion
  95.7 1.4 pad_maximum_fusion.2
  97.1 7.6 %all_to_all.78 = f32[8,1,2]{2,1,0:T(1,128)S(1)} all-to-all(f32[8,1,2]{2,1,0:T(1,128)S(1)} %broadcast_in_dim.45), channel_id=1, replica_groups=mesh['act_0'=4,'act_1'=8,'act_2'=2,'rep'=4] {'act_2','rep'}, dimensions={0} | all-to-all | bytes 128 | tf_op jit(solution)/shard_map/all_to_all | solution.py:33
  104.7 12.8 %all_to_all.79 = f32[32,1,2]{2,1,0:T(1,128)S(1)} all-to-all(f32[32,1,2]{2,1,0:T(1,128)S(1)} %broadcast_in_dim.46), channel_id=1, replica_groups=mesh['act_0'=4,'act_1'=8,'act_2'=2,'rep'=4] {'act_0','act_1'}, dimensions={0} | all-to-all | bytes 512 | tf_op jit(solution)/shard_map/all_to_all | solution.py:33
  117.5 0.6 fusion.14
  120.0 32.8 %all_to_all.80 = f32[64,8,512]{2,1,0:T(8,128)S(1)} all-to-all(f32[64,8,512]{2,1,0:T(8,128)S(1)} %divide_multiply_fusion), channel_id=1, replica_groups=mesh['act_0'=4,'act_1'=8,'act_2'=2,'rep'=4] {'act_0','act_1','act_2'}, dimensions={0} | all-to-all | bytes 2097152 | tf_op jit(solution)/shard_map/all_to_all | solution.py:117
  152.8 10.5 %select_reduce_fusion = (f32[32768]{0:T(1024)S(1)}, f32[32768]{0:T(1024)S(1)}, f32[32768]{0:T(1024)S(1)}, f32[32768]{0:T(1024)S(1)}, f32[32768]{0:T(1024)S(1)}, ...) fusion(s32[8,32768]{1,0:T(8,128)S(1)} %copy-done.1, ...), kind=kLoop, calls=%fused_computation.17 | loop fusion | flops 13828096 | bytes 4456448 | tf_op jit(solution)/shard_map/reduce_sum | solution.py:83
  164.2 1.4 copy-done
  165.7 3.3 %reshape.176 = f32[32,18,2,512]{3,2,0,1:T(2,128)S(1)} reshape(f32[32,18,1024]{2,0,1:T(8,128)} %bitcast.89) | data formatting | bytes 4718592 | tf_op jit(solution)/shard_map/reshape | solution.py:15
  169.0 0.5 copy.19
  169.5 5.6 %all_to_all.81 = f32[2,32,18,512]{3,1,2,0:T(8,128)S(1)} all-to-all(f32[2,32,18,512]{3,1,2,0:T(8,128)S(1)} %copy.19), channel_id=1, replica_groups=mesh['act_0'=4,'act_1'=8,'act_2'=2,'rep'=4] {'act_2'}, dimensions={0} | all-to-all | bytes 4718592 | tf_op jit(solution)/shard_map/all_to_all | solution.py:21
  175.1 1.3 reduce_sum.418
  176.4 2.0 copy.20
  178.4 46.7 %all_to_all.82 = f32[32,18,512]{2,1,0:T(8,128)S(1)} all-to-all(f32[32,18,512]{2,1,0:T(8,128)S(1)} %copy.20), channel_id=1, replica_groups=mesh['act_0'=4,'act_1'=8,'act_2'=2,'rep'=4] {'act_0','act_1'}, dimensions={0} | all-to-all | bytes 2359296 | tf_op jit(solution)/shard_map/all_to_all | solution.py:28
  225.1 0.7 reduce_sum.419
  225.8 1.0 copy.53
  (54 shorter events, 1.9 us)
Async XLA Ops:
  0.6 39.5 %all-to-all-start = ((f32[8,64,512]{2,0,1:T(8,128)}), f32[8,64,512]{2,0,1:T(8,128)S(1)}, u32[]{:S(2)}, u32[]{:S(2)}) async-start(f32[8,64,512]{2,0,1:T(8,128)} %bitcast.90), calls=%async_computation | async-start | bytes 2097152 | tf_op jit(solution)/shard_map/all_to_all | solution.py:94
  52.7 15.0 %all-to-all-start.2 = ((f32[32,1,2]{2,1,0:T(1,128)}), f32[32,1,2]{2,1,0:T(1,128)S(1)}, u32[]{:S(2)}, u32[]{:S(2)}) async-start(f32[32,1,2]{2,1,0:T(1,128)} %broadcast_in_dim.42), calls=%async_computation.2 | async-start | bytes 32768 | tf_op jit(solution)/shard_map/all_to_all | solution.py:33
  119.8 33.0 %copy-start.1 = (s32[8,32768]{1,0:T(8,128)S(1)}, s32[8,32768]{1,0:T(8,128)}, u32[]{:S(2)}) copy-start(s32[8,32768]{1,0:T(8,128)} %param.5) | copy-start | bytes 3145732
  164.2 1.4 copy-start
where the time goes:
time: 229 us; the launch traced here: 228 us
  blocking collectives  135 us (59%)
  waiting for transfers between devices  35.1 us (15%)
  other arithmetic  20.2 us (9%)
  starting transfers between devices  18.1 us (8%)
  local copies, waits for them, and re-layouts  11.3 us (5%)
  between operations  7.81 us (3%)
    all_to_all x5, blocking collectives, copy_for_each(): return lax.all_to_all(copies, axis, split_axis=0, concat_axis=0, tiled=True)  50.3 us
    all_to_all x1, blocking collectives, sum_in_two_steps(): return jnp.sum(lax.all_to_all(own, far, 0, 0, tiled=True), axis=0)  46.7 us
    all_to_all x1, blocking collectives, on_device(): lax.all_to_all(move_draws * probs_rows, ACT, split_axis=0, concat_axis=1,...  32.8 us
    all_to_all x1, waiting for transfers between devices, on_device(): lax.all_to_all(estimated_returns, ACT, split_axis=1, concat_axis=0, tiled...  27.2 us
    all_to_all x1, starting transfers between devices, on_device(): lax.all_to_all(estimated_returns, ACT, split_axis=1, concat_axis=0, tiled...  11.6 us
    reduce_sum x1, other arithmetic, per_action(): jnp.sum(jnp.where(ids_block == k, probs, 0.0), axis=0)  10.5 us
    all_to_all x1, waiting for transfers between devices, copy_for_each(): return lax.all_to_all(copies, axis, split_axis=0, concat_axis=0, tiled=True)  7.92 us
    all_to_all x1, starting transfers between devices, copy_for_each(): return lax.all_to_all(copies, axis, split_axis=0, concat_axis=0, tiled=True)  6.46 us
  transfers between devices with their start and end apart: 2, of which 2 were waited for; matrix products, arithmetic and copies ran while one was open for 0% of the time, Pallas kernels for 0%

commit v1 on v0

--- a/solution.py
+++ b/solution.py
@@ -114,9 +114,12 @@
         centered_returns, lagrange_eta
     )
     probs_rows = exponential_term / partition_total
-    sample_importance = lax.all_to_all(
-        move_draws * probs_rows, ACT, split_axis=0, concat_axis=1, tiled=True
-    )
+    message = move_draws * probs_rows
+    out_arr = jax.lax.axis_size(ACT)
+    heard = jnp.split(message, out_arr, axis=0)
+    v1 = jnp.stack(heard)
+    oldest = jax.lax.all_to_all(v1, ACT, 0, 0)
+    sample_importance = jnp.concatenate(oldest, axis=1)
     goal_distribution = scatter_target(sample_importance / jnp.float32(move_draws), chosen_move_ids)
     return (sample_importance, goal_distribution, jnp.reshape(lagrange_eta, (1,)))
 

time: 229 us -> 229 us (level)
  no operation moved by 1% of the time
where the time goes in v1:
time: 229 us
  blocking collectives  135 us (59%)
  waiting for transfers between devices  35.1 us (15%)
  other arithmetic  20.2 us (9%)
  starting transfers between devices  18.1 us (8%)
  local copies, waits for them, and re-layouts  11.5 us (5%)
  between operations  8.32 us (4%)
    all_to_all x5, blocking collectives, copy_for_each(): return lax.all_to_all(copies, axis, split_axis=0, concat_axis=0, tiled=True)  50.3 us
    all_to_all x1, blocking collectives, sum_in_two_steps(): return jnp.sum(lax.all_to_all(own, far, 0, 0, tiled=True), axis=0)  46.7 us
    all_to_all x1, blocking collectives, on_device(): oldest = jax.lax.all_to_all(v1, ACT, 0, 0)  32.6 us
    all_to_all x1, waiting for transfers between devices, on_device(): lax.all_to_all(estimated_returns, ACT, split_axis=1, concat_axis=0, tiled...  27.2 us
    all_to_all x1, starting transfers between devices, on_device(): lax.all_to_all(estimated_returns, ACT, split_axis=1, concat_axis=0, tiled...  11.6 us
    reduce_sum x1, other arithmetic, per_action(): jnp.sum(jnp.where(ids_block == k, probs, 0.0), axis=0)  10.5 us
    all_to_all x1, waiting for transfers between devices, copy_for_each(): return lax.all_to_all(copies, axis, split_axis=0, concat_axis=0, tiled=True)  7.92 us
    all_to_all x1, starting transfers between devices, copy_for_each(): return lax.all_to_all(copies, axis, split_axis=0, concat_axis=0, tiled=True)  6.46 us
  transfers between devices with their start and end apart: 2, of which 2 were waited for; matrix products, arithmetic and copies ran while one was open for 0% of the time, Pallas kernels for 0%

profile of v1, /device:TPU:32, one launch (start us, length us, event | category | flops | bytes accessed | tf_op | source)
XLA Modules:
  0.0 228.5 jit_solution(10513821680011588671)
XLA Ops:
  0.6 11.6 %all-to-all-start = ((f32[8,64,512]{2,0,1:T(8,128)}), f32[8,64,512]{2,0,1:T(8,128)S(1)}, u32[]{:S(2)}, u32[]{:S(2)}) async-start(f32[8,64,512]{2,0,1:T(8,128)} %bitcast.320), calls=%async_computation | async-start | bytes 2097152 | tf_op jit(solution)/shard_map/all_to_all | solution.py:94
  12.9 27.2 %all-to-all-done = f32[8,64,512]{2,0,1:T(8,128)S(1)} async-done(((f32[8,64,512]{2,0,1:T(8,128)}), f32[8,64,512]{2,0,1:T(8,128)S(1)}, u32[]{:S(2)}, u32[]{:S(2)}) %all-to-all-start) | async-done | bytes 1048608 | tf_op jit(solution)/shard_map/all_to_all | solution.py:94
  40.2 0.3 multiply_reduce_fusion.2
  40.5 0.6 add_reduce_fusion.2
  41.2 1.4 pad_maximum_fusion
  42.5 9.5 %all_to_all.70 = f32[8,1,2]{2,1,0:T(1,128)S(1)} all-to-all(f32[8,1,2]{2,1,0:T(1,128)S(1)} %broadcast_in_dim.41), channel_id=1, replica_groups=mesh['act_0'=4,'act_1'=8,'act_2'=2,'rep'=4] {'act_2','rep'}, dimensions={0} | all-to-all | bytes 128 | tf_op jit(solution)/shard_map/all_to_all | solution.py:33
  52.1 0.6 broadcast_in_dim.42
  52.7 6.5 %all-to-all-start.2 = ((f32[32,1,2]{2,1,0:T(1,128)}), f32[32,1,2]{2,1,0:T(1,128)S(1)}, u32[]{:S(2)}, u32[]{:S(2)}) async-start(f32[32,1,2]{2,1,0:T(1,128)} %broadcast_in_dim.42), calls=%async_computation.2 | async-start | bytes 32768 | tf_op jit(solution)/shard_map/all_to_all | solution.py:33
  59.8 7.9 %all-to-all-done.2 = f32[32,1,2]{2,1,0:T(1,128)S(1)} async-done(((f32[32,1,2]{2,1,0:T(1,128)}), f32[32,1,2]{2,1,0:T(1,128)S(1)}, u32[]{:S(2)}, u32[]{:S(2)}) %all-to-all-start.2) | async-done | bytes 288 | tf_op jit(solution)/shard_map/all_to_all | solution.py:33
  67.8 0.6 fusion.9
  69.8 0.3 multiply_reduce_fusion.1
  70.2 0.6 add_reduce_fusion.1
  70.8 1.4 pad_maximum_fusion.1
  72.2 7.6 %all_to_all.71 = f32[8,1,2]{2,1,0:T(1,128)S(1)} all-to-all(f32[8,1,2]{2,1,0:T(1,128)S(1)} %broadcast_in_dim.43), channel_id=1, replica_groups=mesh['act_0'=4,'act_1'=8,'act_2'=2,'rep'=4] {'act_2','rep'}, dimensions={0} | all-to-all | bytes 128 | tf_op jit(solution)/shard_map/all_to_all | solution.py:33
  79.8 12.8 %all_to_all.72 = f32[32,1,2]{2,1,0:T(1,128)S(1)} all-to-all(f32[32,1,2]{2,1,0:T(1,128)S(1)} %broadcast_in_dim.44), channel_id=1, replica_groups=mesh['act_0'=4,'act_1'=8,'act_2'=2,'rep'=4] {'act_0','act_1'}, dimensions={0} | all-to-all | bytes 512 | tf_op jit(solution)/shard_map/all_to_all | solution.py:33
  92.7 0.6 fusion.8
  95.1 0.6 add_reduce_fusion
  95.7 1.4 pad_maximum_fusion.2
  97.1 7.6 %all_to_all.73 = f32[8,1,2]{2,1,0:T(1,128)S(1)} all-to-all(f32[8,1,2]{2,1,0:T(1,128)S(1)} %broadcast_in_dim.45), channel_id=1, replica_groups=mesh['act_0'=4,'act_1'=8,'act_2'=2,'rep'=4] {'act_2','rep'}, dimensions={0} | all-to-all | bytes 128 | tf_op jit(solution)/shard_map/all_to_all | solution.py:33
  104.7 12.8 %all_to_all.74 = f32[32,1,2]{2,1,0:T(1,128)S(1)} all-to-all(f32[32,1,2]{2,1,0:T(1,128)S(1)} %broadcast_in_dim.46), channel_id=1, replica_groups=mesh['act_0'=4,'act_1'=8,'act_2'=2,'rep'=4] {'act_0','act_1'}, dimensions={0} | all-to-all | bytes 512 | tf_op jit(solution)/shard_map/all_to_all | solution.py:33
  117.5 0.6 fusion.7
  120.8 32.6 %all_to_all.75 = f32[64,8,512]{2,1,0:T(8,128)S(1)} all-to-all(f32[64,8,512]{2,1,0:T(8,128)S(1)} %constant_dynamic-update-slice_fusion), channel_id=1, replica_groups=mesh['act_0'=4,'act_1'=8,'act_2'=2,'rep'=4] {'act_0','act_1','act_2'}, dimensions={0} | all-to-all | bytes 2097152 | tf_op jit(solution)/shard_map/all_to_all | solution.py:121
  153.4 10.5 %select_reduce_fusion = (f32[32768]{0:T(1024)S(1)}, f32[32768]{0:T(1024)S(1)}, f32[32768]{0:T(1024)S(1)}, f32[32768]{0:T(1024)S(1)}, f32[32768]{0:T(1024)S(1)}, ...) fusion(s32[8,32768]{1,0:T(8,128)S(1)} %copy-done.1, ...), kind=kLoop, calls=%fused_computation.6 | loop fusion | flops 13828096 | bytes 4456448 | tf_op jit(solution)/shard_map/reduce_sum | solution.py:83
  164.9 1.4 copy-done
  166.3 3.3 %reshape.171 = f32[32,18,2,512]{3,2,0,1:T(2,128)S(1)} reshape(f32[32,18,1024]{2,0,1:T(8,128)} %bitcast.319) | data formatting | bytes 4718592 | tf_op jit(solution)/shard_map/reshape | solution.py:15
  169.6 0.5 copy.19
  170.1 5.6 %all_to_all.76 = f32[2,32,18,512]{3,1,2,0:T(8,128)S(1)} all-to-all(f32[2,32,18,512]{3,1,2,0:T(8,128)S(1)} %copy.19), channel_id=1, replica_groups=mesh['act_0'=4,'act_1'=8,'act_2'=2,'rep'=4] {'act_2'}, dimensions={0} | all-to-all | bytes 4718592 | tf_op jit(solution)/shard_map/all_to_all | solution.py:21
  175.7 1.3 reduce_sum.418
  177.0 2.0 copy.20
  179.0 46.7 %all_to_all.77 = f32[32,18,512]{2,1,0:T(8,128)S(1)} all-to-all(f32[32,18,512]{2,1,0:T(8,128)S(1)} %copy.20), channel_id=1, replica_groups=mesh['act_0'=4,'act_1'=8,'act_2'=2,'rep'=4] {'act_0','act_1'}, dimensions={0} | all-to-all | bytes 2359296 | tf_op jit(solution)/shard_map/all_to_all | solution.py:28
  225.7 0.7 reduce_sum.419
  226.4 1.0 copy.116
  (118 shorter events, 2.1 us)
Async XLA Ops:
  0.6 39.5 %all-to-all-start = ((f32[8,64,512]{2,0,1:T(8,128)}), f32[8,64,512]{2,0,1:T(8,128)S(1)}, u32[]{:S(2)}, u32[]{:S(2)}) async-start(f32[8,64,512]{2,0,1:T(8,128)} %bitcast.320), calls=%async_computation | async-start | bytes 2097152 | tf_op jit(solution)/shard_map/all_to_all | solution.py:94
  52.7 15.0 %all-to-all-start.2 = ((f32[32,1,2]{2,1,0:T(1,128)}), f32[32,1,2]{2,1,0:T(1,128)S(1)}, u32[]{:S(2)}, u32[]{:S(2)}) async-start(f32[32,1,2]{2,1,0:T(1,128)} %broadcast_in_dim.42), calls=%async_computation.2 | async-start | bytes 32768 | tf_op jit(solution)/shard_map/all_to_all | solution.py:33
  120.0 33.4 %copy-start.1 = (s32[8,32768]{1,0:T(8,128)S(1)}, s32[8,32768]{1,0:T(8,128)}, u32[]{:S(2)}) copy-start(s32[8,32768]{1,0:T(8,128)} %param.5) | copy-start | bytes 3145732
  164.8 1.4 copy-start
